TPU v7x, 32 devices: a whole 2x2x4 slice. The times are simulated.
32 devices in a mesh: pa: 16 (over z, y, core), pb: 2 (over x).
Axes of the slice: x: 2, y: 2, z: 4, core: 2. Of those that a mesh axis runs over, the one named last changes fastest.
Arguments:
- sources: float32 [4096, 128], P(('pa', 'pb')), may hold values from -3 to 3, as said below
- targets: bfloat16 [4096, 128], P(('pa', 'pb')), may hold values from -2 to 2, as said below
- source_mass: float32 [4096], P(('pa', 'pb')), may hold values from -1 to 1
- target_mass: float32 [4096], P(('pa', 'pb')), may hold values from -1 to 1
Outputs:
- moved: float32 [4096, 128], P(('pa', 'pb'))
- dual_source: float32 [4096], P(('pa', 'pb'))
- dual_target: float32 [4096], P(('pa', 'pb'))
Inputs may be any that keep to these rules, and one draw needn't show every extreme that they name: `targets`: each block of 128 target rows is drawn around one cluster centre, a different one for each block. `sources`: each block of 128 source rows is drawn around a cluster centre of its own, drawn independently of the target centres, possibly offset by a common shift.
All inputs are finite; a program needn't handle non-finite values.
Results may differ from a plain program's by a relative error of at most 0.003.
Values may be sent and summed in bfloat16 or wider, within the bound.
A program may use at most 64 MiB of HBM per device.

v0:
```python
from functools import partial
import jax
import jax.numpy as jnp
from jax import lax
from jax.sharding import PartitionSpec as P

STEPS = 1
ITERS = 2
step_rate = 0.25
floor_value = -1e30


def merged(part, axis, combine):
    gathered = jax.tree.map(lambda a: lax.all_gather(a, axis), part)

    def take(source):
        return jax.tree.map(lambda a: lax.dynamic_index_in_dim(a, source, 0, False), gathered)

    return lax.fori_loop(
        1, lax.axis_size(axis), lambda source, state: combine(state, take(source)), take(0)
    )


def squares(coords):
    wide = coords.astype(jnp.float32)
    return jnp.sum(wide * wide, axis=1)


def pair_cost(left, left_norm, right, right_norm):
    inner = lax.dot_general(
        left, right, (((1,), (1,)), ((), ())), preferred_element_type=jnp.float32
    )
    return left_norm[:, None] + right_norm[None, :] - 2.0 * inner


def over_blocks(update, carry, total):
    block_width = 512 if total % 512 == 0 else total
    block_count = total // block_width
    if block_count == 1:
        return update(carry, 0, block_width)
    return lax.fori_loop(
        0,
        block_count,
        lambda position, current: update(current, position * block_width, block_width),
        carry,
    )


def lse_piece(rows, row_norm, columns, column_norm, carry, piece, start):

    def update(current, offset, length):
        chosen = lax.dynamic_slice_in_dim(columns, start + offset, length, 0)
        chosen_norm = lax.dynamic_slice_in_dim(column_norm, start + offset, length, 0)
        values = lax.dynamic_slice_in_dim(piece, offset, length, 0)
        scores = values[None, :] - pair_cost(rows, row_norm, chosen, chosen_norm)
        highest, totals = current
        raised = jnp.maximum(highest, jnp.max(scores, axis=1))
        totals = totals * jnp.exp(highest - raised) + jnp.sum(
            jnp.exp(scores - raised[:, None]), axis=1
        )
        return (raised, totals)

    return over_blocks(update, carry, piece.shape[0])


def plan_piece(rows, row_norm, row_pot, columns, column_norm, carry, piece, start):

    def update(current, offset, length):
        chosen = lax.dynamic_slice_in_dim(columns, start + offset, length, 0)
        chosen_norm = lax.dynamic_slice_in_dim(column_norm, start + offset, length, 0)
        values = lax.dynamic_slice_in_dim(piece, offset, length, 0)
        cost = pair_cost(rows, row_norm, chosen, chosen_norm)
        weights = jnp.exp(row_pot[:, None] + values[None, :] - cost).astype(jnp.bfloat16)
        return current + jnp.dot(weights, chosen, preferred_element_type=jnp.float32)

    return over_blocks(update, carry, piece.shape[0])


def join_lse(first, second):
    raised = jnp.maximum(first[0], second[0])
    return (raised, first[1] * jnp.exp(first[0] - raised) + second[1] * jnp.exp(second[0] - raised))


def start_lse(length):
    return (jnp.full((length,), floor_value, jnp.float32), jnp.zeros((length,), jnp.float32))


def finish(carry):
    return -(carry[0] + jnp.log(carry[1]))


def body(sources, targets, source_mass, target_mass):
    own_rows = sources.shape[0]
    own_targets = targets.shape[0]
    target_norm = squares(targets)
    moving = sources
    dual_target = jnp.zeros((own_targets,), jnp.float32)
    dual_source = jnp.zeros((own_rows,), jnp.float32)
    member = lax.axis_index("pb")
    half_targets = lax.all_gather(targets, "pa", axis=0, tiled=True)
    half_norm = squares(half_targets)
    pair_mass = lax.all_gather(source_mass, "pb", axis=0, tiled=True)
    pair_dual = jnp.zeros((pair_mass.shape[0],), jnp.float32)
    for flow_step in range(STEPS):
        coarse = moving.astype(jnp.bfloat16)
        pair_coarse = lax.all_gather(coarse, "pb", axis=0, tiled=True)
        pair_norm = squares(pair_coarse)
        pair_count = pair_coarse.shape[0]
        all_sources = lax.all_gather(pair_coarse, "pa", axis=0, tiled=True)
        all_source_norm = squares(all_sources)
        row_fold = partial(lse_piece, pair_coarse, pair_norm, half_targets, half_norm)
        column_fold = partial(lse_piece, targets, target_norm, all_sources, all_source_norm)
        shifted = dual_target + target_mass
        for sweep in range(ITERS + 1):
            shifted = dual_target + target_mass
            half_lse = row_fold(
                start_lse(pair_count),
                jax.tree.map(lambda part: lax.all_gather(part, "pa", axis=0, tiled=True), shifted),
                jnp.int32(0),
            )
            pair_dual = finish(merged((half_lse[0], half_lse[1]), "pb", join_lse))
            if sweep < ITERS:
                lifted = pair_dual + pair_mass
                dual_target = finish(
                    column_fold(
                        start_lse(own_targets),
                        jax.tree.map(
                            lambda part: lax.all_gather(part, "pa", axis=0, tiled=True), lifted
                        ),
                        jnp.int32(0),
                    )
                )
        plan_fold = partial(plan_piece, pair_coarse, pair_norm, pair_dual, half_targets, half_norm)
        empty = jnp.zeros((pair_count, sources.shape[1]), jnp.float32)
        pair_centre = plan_fold(
            empty,
            jax.tree.map(lambda part: lax.all_gather(part, "pa", axis=0, tiled=True), shifted),
            jnp.int32(0),
        )
        centre = lax.psum_scatter(
            pair_centre.astype(jnp.bfloat16), "pb", scatter_dimension=0, tiled=True
        ).astype(jnp.float32)
        moving = moving - 2.0 * step_rate * (moving - centre)
    dual_source = lax.dynamic_slice_in_dim(pair_dual, member * own_rows, own_rows, 0)
    return (moving, dual_source, dual_target)


def solution(mesh):
    return jax.shard_map(
        body,
        mesh=mesh,
        in_specs=(P(("pa", "pb"), None), P(("pa", "pb"), None), P(("pa", "pb")), P(("pa", "pb"))),
        out_specs=(P(("pa", "pb"), None), P(("pa", "pb")), P(("pa", "pb"))),
        check_vma=False,
    )
```

profile of v0, /device:TPU:0, one launch (start us, length us, event | category | flops | bytes accessed | tf_op | source)
XLA Modules:
  0.0 212.0 jit_solution(4313513718906820735)
XLA Ops:
  8.1 5.6 %all_gather.65 = bf16[256,128]{1,0:T(8,128)(2,1)} all-gather(bf16[128,128]{1,0:T(8,128)(2,1)S(1)} %convert_element_type.28), channel_id=1, replica_groups=mesh['pa'=16,'pb'=2] {'pb'}, dimensions={0}, use_global_device_ids=true | all-gather | bytes 98304 | tf_op jit(solution)/shard_map/all_gather | solution.py:106
  14.7 24.4 %all_gather.66 = bf16[2048,128]{1,0:T(8,128)(2,1)S(1)} all-gather(bf16[128,128]{1,0:T(8,128)(2,1)} %param.17), channel_id=1, replica_groups=mesh['pa'=16,'pb'=2] {'pa'}, dimensions={0}, use_global_device_ids=true | all-gather | bytes 557056 | tf_op jit(solution)/shard_map/all_gather | solution.py:100
  39.4 17.5 %all-gather.6 = f32[16,1,128]{2,1,0:T(1,128)S(1)} all-gather(f32[1,1,128]{2,1,0:T(1,128)S(1)} %bitcast.107), channel_id=1, replica_groups=mesh['pa'=16,'pb'=2] {'pa'}, dimensions={0}, use_global_device_ids=true | all-gather | bytes 8704 | tf_op jit(solution)/shard_map/all_gather | solution.py:118
  56.9 2.4 %while.112 = (s32[]{:T(128)}, f32[256]{0:T(256)S(1)}, f32[256]{0:T(256)S(1)}, f32[2048]{0:T(1024)S(1)}, f32[256]{0:T(256)S(1)}, /*index=5*/f32[2048]{0:T(1024)S(...) while((s32[]{:T(128)}, f32[256]{0:T(256)S(1)}, ...), condition=%wide.region_6.7_spmd.clone, body=%wide.region_3.6_spmd.clone.sunk | while | flops 34473220 | bytes 1271994 | solution.py:41
  59.4 4.2 %all-gather.9 = f32[2,1,128]{2,1,0:T(1,128)S(1)} all-gather(f32[1,1,128]{2,1,0:T(1,128)S(1)} %bitcast.124), channel_id=1, replica_groups=mesh['pa'=16,'pb'=2] {'pb'}, dimensions={0}, use_global_device_ids=true | all-gather | bytes 1536 | tf_op jit(solution)/shard_map/all_gather | solution.py:102
  63.7 4.2 %all-gather.7 = f32[2,1,256]{2,1,0:T(1,128)S(1)} all-gather(f32[1,1,256]{2,1,0:T(1,128)S(1)} %bitcast.98), channel_id=2, replica_groups=mesh['pa'=16,'pb'=2] {'pb'}, dimensions={0}, use_global_device_ids=true | all-gather | bytes 3072 | tf_op jit(solution)/shard_map/all_gather | solution.py:14
  67.9 4.2 %all-gather.8 = f32[2,1,256]{2,1,0:T(1,128)S(1)} all-gather(f32[1,1,256]{2,1,0:T(1,128)S(1)} %bitcast.106), channel_id=3, replica_groups=mesh['pa'=16,'pb'=2] {'pb'}, dimensions={0}, use_global_device_ids=true | all-gather | bytes 3072 | tf_op jit(solution)/shard_map/all_gather | solution.py:14
  72.2 18.8 %all-gather.10 = f32[16,1,256]{2,1,0:T(1,128)S(1)} all-gather(f32[1,1,256]{2,1,0:T(1,128)S(1)} %bitcast.113), channel_id=1, replica_groups=mesh['pa'=16,'pb'=2] {'pa'}, dimensions={0}, use_global_device_ids=true | all-gather | bytes 17408 | tf_op jit(solution)/shard_map/all_gather | solution.py:128
  91.2 1.8 multiply_reduce_fusion
  93.0 11.5 %while.113 = (s32[]{:T(128)}, f32[128]{0:T(128)S(1)}, f32[128]{0:T(128)S(1)}, f32[4096]{0:T(1024)S(1)}, f32[128]{0:T(128)S(1)}, /*index=5*/f32[4096]{0:T(1024)S(...) while((s32[]{:T(128)}, f32[128]{0:T(128)S(1)}, ...), condition=%wide.region_11.0_spmd.clone, body=%wide.region_8.11_spmd.clone.sunk | while | flops 17236612 | bytes 707770 | solution.py:41
  93.2 1.1 fusion.108
  94.6 1.1 fusion.108
  96.1 1.1 fusion.108
  98.9 1.1 fusion.108
  100.4 1.1 fusion.108
  104.6 17.4 %all-gather.11 = f32[16,1,128]{2,1,0:T(1,128)S(1)} all-gather(f32[1,1,128]{2,1,0:T(1,128)S(1)} %add_bitcast_fusion.1), channel_id=1, replica_groups=mesh['pa'=16,'pb'=2] {'pa'}, dimensions={0}, use_global_device_ids=true | all-gather | bytes 8704 | tf_op jit(solution)/shard_map/all_gather | solution.py:118
  122.0 2.4 %while.114 = (s32[]{:T(128)}, f32[256]{0:T(256)S(1)}, f32[256]{0:T(256)S(1)}, f32[2048]{0:T(1024)S(1)}, f32[256]{0:T(256)S(1)}, /*index=5*/f32[2048]{0:T(1024)S(...) while((s32[]{:T(128)}, f32[256]{0:T(256)S(1)}, ...), condition=%wide.region_15.0_spmd.clone, body=%wide.region_12.15_spmd.clone.sunk | while | flops 34473220 | bytes 1271994 | solution.py:41
  124.4 4.2 %all-gather.12 = f32[2,1,256]{2,1,0:T(1,128)S(1)} all-gather(f32[1,1,256]{2,1,0:T(1,128)S(1)} %bitcast.97), channel_id=4, replica_groups=mesh['pa'=16,'pb'=2] {'pb'}, dimensions={0}, use_global_device_ids=true | all-gather | bytes 3072 | tf_op jit(solution)/shard_map/all_gather | solution.py:14
  128.7 4.2 %all-gather.13 = f32[2,1,256]{2,1,0:T(1,128)S(1)} all-gather(f32[1,1,256]{2,1,0:T(1,128)S(1)} %bitcast.105), channel_id=5, replica_groups=mesh['pa'=16,'pb'=2] {'pb'}, dimensions={0}, use_global_device_ids=true | all-gather | bytes 3072 | tf_op jit(solution)/shard_map/all_gather | solution.py:14
  132.9 18.8 %all-gather.14 = f32[16,1,256]{2,1,0:T(1,128)S(1)} all-gather(f32[1,1,256]{2,1,0:T(1,128)S(1)} %bitcast.112), channel_id=1, replica_groups=mesh['pa'=16,'pb'=2] {'pa'}, dimensions={0}, use_global_device_ids=true | all-gather | bytes 17408 | tf_op jit(solution)/shard_map/all_gather | solution.py:128
  151.7 11.5 %while.115 = (s32[]{:T(128)}, f32[128]{0:T(128)S(1)}, f32[128]{0:T(128)S(1)}, f32[4096]{0:T(1024)S(1)}, f32[128]{0:T(128)S(1)}, /*index=5*/f32[4096]{0:T(1024)S(...) while((s32[]{:T(128)}, f32[128]{0:T(128)S(1)}, ...), condition=%wide.region_19.20_spmd.clone, body=%wide.region_16.19_spmd.clone.sunk | while | flops 17236612 | bytes 707770 | solution.py:41
  151.9 1.1 fusion.116
  159.1 1.1 fusion.116
  160.5 1.1 fusion.116
  162.0 1.1 fusion.116
  163.8 17.4 %all-gather.15 = f32[16,1,128]{2,1,0:T(1,128)S(1)} all-gather(f32[1,1,128]{2,1,0:T(1,128)S(1)} %get-tuple-element.1165), channel_id=1, replica_groups=mesh['pa'=16,'pb'=2] {'pa'}, dimensions={0}, use_global_device_ids=true | all-gather | bytes 8704 | tf_op jit(solution)/shard_map/all_gather | solution.py:137
  181.2 2.4 %while.116 = (s32[]{:T(128)}, f32[256]{0:T(256)S(1)}, f32[256]{0:T(256)S(1)}, f32[2048]{0:T(1024)S(1)}, f32[256]{0:T(256)S(1)}, /*index=5*/f32[2048]{0:T(1024)S(...) while((s32[]{:T(128)}, f32[256]{0:T(256)S(1)}, ...), condition=%wide.region_23.24_spmd.clone, body=%wide.region_20.23_spmd.clone.sunk | while | flops 34473220 | bytes 1271994 | solution.py:41
  183.6 4.2 %all-gather.16 = f32[2,1,256]{2,1,0:T(1,128)S(1)} all-gather(f32[1,1,256]{2,1,0:T(1,128)S(1)} %bitcast.96), channel_id=6, replica_groups=mesh['pa'=16,'pb'=2] {'pb'}, dimensions={0}, use_global_device_ids=true | all-gather | bytes 3072 | tf_op jit(solution)/shard_map/all_gather | solution.py:14
  187.9 4.2 %all-gather.17 = f32[2,1,256]{2,1,0:T(1,128)S(1)} all-gather(f32[1,1,256]{2,1,0:T(1,128)S(1)} %bitcast.104), channel_id=7, replica_groups=mesh['pa'=16,'pb'=2] {'pb'}, dimensions={0}, use_global_device_ids=true | all-gather | bytes 3072 | tf_op jit(solution)/shard_map/all_gather | solution.py:14
  192.1 2.4 %while.117 = (s32[]{:T(128)}, f32[256,128]{1,0:T(8,128)S(1)}, f32[256]{0:T(256)S(1)}, f32[2048]{0:T(1024)S(1)}, f32[256]{0:T(256)S(1)}, /*index=5*/f32[2048]{0:T...) while((s32[]{:T(128)}, f32[256,128]{1,0:T(8,128)S(1)}, ...), condition=%wide.region_25.0_spmd.clone, body=%wide.region_24.25_spmd.clone.sunk | while | flops 67960840 | bytes 605876 | solution.py:41
  195.8 8.0 %reduce-scatter.2.cloned.1.call-done = bf16[128,128]{1,0:T(8,128)(2,1)} async-done(((bf16[256,128]{1,0:T(8,128)(2,1)}), bf16[128,128]{1,0:T(8,128)(2,1)}) %reduce-scatter.2.cloned.1.call-update) | async-done | bytes 32784 | tf_op jit(solution)/shard_map/reduce_scatter | solution.py:140
  203.7 1.4 multiply_subtract_fusion
  (242 shorter events, 25.6 us)
Async XLA Ops:
  7.2 32.3 %copy-start.3 = (f32[128]{0:T(128)S(1)}, f32[128]{0:T(128)}, u32[]{:S(2)}) copy-start(f32[128]{0:T(128)} %param.19) | copy-start | bytes 1540
  7.2 84.0 %all-gather.20.cloned.1.call-start = ((), (), s32[]{:S(2)}) async-start(), calls=%async_computation.1 | async-start | bytes 1114112 | tf_op jit(solution)/shard_map/all_gather | solution.py:109
  13.7 43.2 %copy-start = (bf16[256,128]{1,0:T(8,128)(2,1)S(1)}, bf16[256,128]{1,0:T(8,128)(2,1)}, u32[]{:S(2)}) copy-start(bf16[256,128]{1,0:T(8,128)(2,1)} %all_gather.65) | copy-start | bytes 196612
  13.7 190.0 %reduce-scatter.2.cloned.1.call-start = ((), (), s32[]{:S(2)}) async-start(), calls=%async_computation.2 | async-start | bytes 98304 | tf_op jit(solution)/shard_map/reduce_scatter | solution.py:140
  56.9 2.5 %copy-start.4 = (f32[128]{0:T(128)S(1)}, f32[128]{0:T(128)}, u32[]{:S(2)}) copy-start(f32[128]{0:T(128)} %param.18) | copy-start | bytes 1540
  56.9 34.1 %copy-start.2 = (bf16[128,128]{1,0:T(8,128)(2,1)S(1)}, bf16[128,128]{1,0:T(8,128)(2,1)}, u32[]{:S(2)}) copy-start(bf16[128,128]{1,0:T(8,128)(2,1)} %param.17) | copy-start | bytes 98308
  192.1 11.6 %copy-start.1 = (f32[128,128]{1,0:T(8,128)S(1)}, f32[128,128]{1,0:T(8,128)}, u32[]{:S(2)}) copy-start(f32[128,128]{1,0:T(8,128)} %param.16) | copy-start | bytes 196612
Sparse Core Ops, SparseCore 0:
  13.8 40.4 all-gather.19
  195.3 8.3 reduce-scatter.1
where the time goes:
time: 213 us; the launch traced here: 212 us
  blocking collectives  150 us (70%)
  matrix products  23.1 us (11%)
  between operations  14.3 us (7%)
  other arithmetic  10.3 us (5%)
  waiting for transfers between devices  8.02 us (4%)
  local copies, waits for them, and re-layouts  5.52 us (3%)
    all_gather x5, blocking collectives, body(): lax.all_gather(part, 'pa', axis=0, tiled=True)  90 us
    all_gather x6, blocking collectives, merged(): gathered = jax.tree.map(lambda a: lax.all_gather(a, axis), part)  25.4 us
    all_gather x1, blocking collectives, body(): half_targets = lax.all_gather(targets, 'pa', axis=0, tiled=True)  24.4 us
    dot_general x28, matrix products, pair_cost(): lax.dot_general(left, right, (((1,), (1,)), ((), ())), preferred_element_...  21.5 us
    reduce_scatter x1, waiting for transfers between devices, body(): lax.psum_scatter(pair_centre.astype(jnp.bfloat16), 'pb', scatter_dimensio...  7.97 us
    all_gather x1, blocking collectives, body(): pair_coarse = lax.all_gather(coarse, 'pb', axis=0, tiled=True)  5.6 us
  transfers between devices with their start and end apart: 2, of which 1 were waited for; matrix products, arithmetic and copies ran while one was open for 2% of the time, Pallas kernels for 0%

commit v1 on v0

--- a/solution.py
+++ b/solution.py
@@ -97,7 +97,12 @@
     dual_target = jnp.zeros((own_targets,), jnp.float32)
     dual_source = jnp.zeros((own_rows,), jnp.float32)
     member = lax.axis_index("pb")
-    half_targets = lax.all_gather(targets, "pa", axis=0, tiled=True)
+    ring = [targets]
+    for hop in range(15):
+        ring.append(lax.ppermute(ring[-1], "pa", [(dev, (dev + 1) % 16) for dev in range(16)]))
+    half_targets = jnp.roll(
+        jnp.concatenate(ring[::-1], axis=0), (lax.axis_index("pa") + 1) * ring[0].shape[0], axis=0
+    )
     half_norm = squares(half_targets)
     pair_mass = lax.all_gather(source_mass, "pb", axis=0, tiled=True)
     pair_dual = jnp.zeros((pair_mass.shape[0],), jnp.float32)

time: 213 us -> 269 us (1.26)
  waiting for transfers between devices: 8.02 us -> 87.1 us
  blocking collectives: 150 us -> 125 us
    ppermute x0 -> x15, waiting for transfers between devices: none -> 78.7 us  [body(): lax.ppermute(ring[-1], 'pa', [(dev, (dev + 1) % 16) for dev in range(16)])]
    all_gather x1 -> x0, blocking collectives: 24.4 us -> none  [body(): half_targets = lax.all_gather(targets, 'pa', axis=0, tiled=True)]
  transfers between devices with their start and end apart: 2 -> 17, of which waited for: 1 -> 15; matrix products, arithmetic and copies ran while one was open for 2% -> 2% of each run, Pallas kernels for 0% -> 0%
where the time goes in v1:
time: 269 us; the launch traced here: 268 us
  blocking collectives  125 us (46%)
  waiting for transfers between devices  87.1 us (32%)
  matrix products  23.2 us (9%)
  between operations  14.5 us (5%)
  other arithmetic  11.1 us (4%)
  local copies, waits for them, and re-layouts  6.07 us (2%)
    all_gather x5, blocking collectives, body(): lax.all_gather(part, 'pa', axis=0, tiled=True)  90.1 us
    ppermute x15, waiting for transfers between devices, body(): lax.ppermute(ring[-1], 'pa', [(dev, (dev + 1) % 16) for dev in range(16)])  78.7 us
    all_gather x6, blocking collectives, merged(): gathered = jax.tree.map(lambda a: lax.all_gather(a, axis), part)  25.4 us
    dot_general x28, matrix products, pair_cost(): lax.dot_general(left, right, (((1,), (1,)), ((), ())), preferred_element_...  21.5 us
    reduce_scatter x1, waiting for transfers between devices, body(): lax.psum_scatter(pair_centre.astype(jnp.bfloat16), 'pb', scatter_dimensio...  8.39 us
  transfers between devices with their start and end apart: 17, of which 15 were waited for; matrix products, arithmetic and copies ran while one was open for 2% of the time, Pallas kernels for 0%

profile of v1, /device:TPU:0, one launch (start us, length us, event | category | flops | bytes accessed | tf_op | source)
XLA Modules:
  0.0 268.1 jit_solution(1985289216560657253)
XLA Ops:
  7.8 6.8 %collective-permute-done = bf16[128,128]{1,0:T(8,128)(2,1)S(1)} collective-permute-done((bf16[128,128]{1,0:T(8,128)(2,1)}, bf16[128,128]{1,0:T(8,128)(2,1)S(1)}, u32[]{:S(2)}, u32[]{:S(2)}) %collective-permute-start) | collective-permute-done | bytes 32800 | tf_op jit(solution)/shard_map/ppermute | solution.py:102
  14.6 6.0 %collective-permute-done.1 = bf16[128,128]{1,0:T(8,128)(2,1)S(1)} collective-permute-done((bf16[128,128]{1,0:T(8,128)(2,1)S(1)}, bf16[128,128]{1,0:T(8,128)(2,1)S(1)}, u32[]{:S(2)}, u32[]{:S(2)}) %collective-permute-start.1) | collective-permute-done | bytes 32800 | tf_op jit(solution)/shard_map/ppermute | solution.py:102
  20.6 6.0 %collective-permute-done.2 = bf16[128,128]{1,0:T(8,128)(2,1)S(1)} collective-permute-done((bf16[128,128]{1,0:T(8,128)(2,1)S(1)}, bf16[128,128]{1,0:T(8,128)(2,1)S(1)}, u32[]{:S(2)}, u32[]{:S(2)}) %collective-permute-start.2) | collective-permute-done | bytes 32800 | tf_op jit(solution)/shard_map/ppermute | solution.py:102
  26.6 6.0 %collective-permute-done.3 = bf16[128,128]{1,0:T(8,128)(2,1)S(1)} collective-permute-done((bf16[128,128]{1,0:T(8,128)(2,1)S(1)}, bf16[128,128]{1,0:T(8,128)(2,1)S(1)}, u32[]{:S(2)}, u32[]{:S(2)}) %collective-permute-start.3) | collective-permute-done | bytes 32800 | tf_op jit(solution)/shard_map/ppermute | solution.py:102
  32.7 6.0 %collective-permute-done.4 = bf16[128,128]{1,0:T(8,128)(2,1)S(1)} collective-permute-done((bf16[128,128]{1,0:T(8,128)(2,1)S(1)}, bf16[128,128]{1,0:T(8,128)(2,1)S(1)}, u32[]{:S(2)}, u32[]{:S(2)}) %collective-permute-start.4) | collective-permute-done | bytes 32800 | tf_op jit(solution)/shard_map/ppermute | solution.py:102
  38.7 6.0 %collective-permute-done.5 = bf16[128,128]{1,0:T(8,128)(2,1)S(1)} collective-permute-done((bf16[128,128]{1,0:T(8,128)(2,1)S(1)}, bf16[128,128]{1,0:T(8,128)(2,1)S(1)}, u32[]{:S(2)}, u32[]{:S(2)}) %collective-permute-start.5) | collective-permute-done | bytes 32800 | tf_op jit(solution)/shard_map/ppermute | solution.py:102
  44.7 6.0 %collective-permute-done.6 = bf16[128,128]{1,0:T(8,128)(2,1)S(1)} collective-permute-done((bf16[128,128]{1,0:T(8,128)(2,1)S(1)}, bf16[128,128]{1,0:T(8,128)(2,1)S(1)}, u32[]{:S(2)}, u32[]{:S(2)}) %collective-permute-start.6) | collective-permute-done | bytes 32800 | tf_op jit(solution)/shard_map/ppermute | solution.py:102
  50.8 6.0 %collective-permute-done.7 = bf16[128,128]{1,0:T(8,128)(2,1)S(1)} collective-permute-done((bf16[128,128]{1,0:T(8,128)(2,1)S(1)}, bf16[128,128]{1,0:T(8,128)(2,1)S(1)}, u32[]{:S(2)}, u32[]{:S(2)}) %collective-permute-start.7) | collective-permute-done | bytes 32800 | tf_op jit(solution)/shard_map/ppermute | solution.py:102
  56.8 6.0 %collective-permute-done.8 = bf16[128,128]{1,0:T(8,128)(2,1)S(1)} collective-permute-done((bf16[128,128]{1,0:T(8,128)(2,1)S(1)}, bf16[128,128]{1,0:T(8,128)(2,1)S(1)}, u32[]{:S(2)}, u32[]{:S(2)}) %collective-permute-start.8) | collective-permute-done | bytes 32800 | tf_op jit(solution)/shard_map/ppermute | solution.py:102
  62.9 6.0 %collective-permute-done.9 = bf16[128,128]{1,0:T(8,128)(2,1)S(1)} collective-permute-done((bf16[128,128]{1,0:T(8,128)(2,1)S(1)}, bf16[128,128]{1,0:T(8,128)(2,1)S(1)}, u32[]{:S(2)}, u32[]{:S(2)}) %collective-permute-start.9) | collective-permute-done | bytes 32800 | tf_op jit(solution)/shard_map/ppermute | solution.py:102
  68.9 6.0 %collective-permute-done.10 = bf16[128,128]{1,0:T(8,128)(2,1)S(1)} collective-permute-done((bf16[128,128]{1,0:T(8,128)(2,1)S(1)}, bf16[128,128]{1,0:T(8,128)(2,1)S(1)}, u32[]{:S(2)}, u32[]{:S(2)}) %collective-permute-start.10) | collective-permute-done | bytes 32800 | tf_op jit(solution)/shard_map/ppermute | solution.py:102
  74.9 6.0 %collective-permute-done.11 = bf16[128,128]{1,0:T(8,128)(2,1)S(1)} collective-permute-done((bf16[128,128]{1,0:T(8,128)(2,1)S(1)}, bf16[128,128]{1,0:T(8,128)(2,1)S(1)}, u32[]{:S(2)}, u32[]{:S(2)}) %collective-permute-start.11) | collective-permute-done | bytes 32800 | tf_op jit(solution)/shard_map/ppermute | solution.py:102
  81.8 4.7 %all_gather.62 = bf16[256,128]{1,0:T(8,128)(2,1)} all-gather(bf16[128,128]{1,0:T(8,128)(2,1)S(1)} %convert_element_type.28), channel_id=1, replica_groups=mesh['pa'=16,'pb'=2] {'pb'}, dimensions={0}, use_global_device_ids=true | all-gather | bytes 98304 | tf_op jit(solution)/shard_map/all_gather | solution.py:111
  88.0 5.1 %collective-permute-done.13 = bf16[128,128]{1,0:T(8,128)(2,1)S(1)} collective-permute-done((bf16[128,128]{1,0:T(8,128)(2,1)S(1)}, bf16[128,128]{1,0:T(8,128)(2,1)S(1)}, u32[]{:S(2)}, u32[]{:S(2)}) %collective-permute-start.13) | collective-permute-done | bytes 32800 | tf_op jit(solution)/shard_map/ppermute | solution.py:102
  94.0 4.4 %all-gather.9 = f32[2,1,128]{2,1,0:T(1,128)S(1)} all-gather(f32[1,1,128]{2,1,0:T(1,128)} %bitcast.124), channel_id=1, replica_groups=mesh['pa'=16,'pb'=2] {'pb'}, dimensions={0}, use_global_device_ids=true | all-gather | bytes 1536 | tf_op jit(solution)/shard_map/all_gather | solution.py:107
  98.4 17.3 %all-gather.6 = f32[16,1,128]{2,1,0:T(1,128)S(1)} all-gather(f32[1,1,128]{2,1,0:T(1,128)} %bitcast.107), channel_id=1, replica_groups=mesh['pa'=16,'pb'=2] {'pa'}, dimensions={0}, use_global_device_ids=true | all-gather | bytes 8704 | tf_op jit(solution)/shard_map/all_gather | solution.py:123
  116.8 2.4 while.112
  119.3 4.2 %all-gather.7 = f32[2,1,256]{2,1,0:T(1,128)S(1)} all-gather(f32[1,1,256]{2,1,0:T(1,128)S(1)} %bitcast.98), channel_id=2, replica_groups=mesh['pa'=16,'pb'=2] {'pb'}, dimensions={0}, use_global_device_ids=true | all-gather | bytes 3072 | tf_op jit(solution)/shard_map/all_gather | solution.py:14
  123.5 4.2 %all-gather.8 = f32[2,1,256]{2,1,0:T(1,128)S(1)} all-gather(f32[1,1,256]{2,1,0:T(1,128)S(1)} %bitcast.106), channel_id=3, replica_groups=mesh['pa'=16,'pb'=2] {'pb'}, dimensions={0}, use_global_device_ids=true | all-gather | bytes 3072 | tf_op jit(solution)/shard_map/all_gather | solution.py:14
  127.8 19.0 %all-gather.10 = f32[16,1,256]{2,1,0:T(1,128)S(1)} all-gather(f32[1,1,256]{2,1,0:T(1,128)S(1)} %bitcast.113), channel_id=1, replica_groups=mesh['pa'=16,'pb'=2] {'pa'}, dimensions={0}, use_global_device_ids=true | all-gather | bytes 17408 | tf_op jit(solution)/shard_map/all_gather | solution.py:133
  148.7 11.5 %while.113 = (s32[]{:T(128)}, f32[128]{0:T(128)S(1)}, f32[128]{0:T(128)S(1)}, f32[4096]{0:T(1024)S(1)}, f32[128]{0:T(128)S(1)}, /*index=5*/f32[4096]{0:T(1024)S(...) while((s32[]{:T(128)}, f32[128]{0:T(128)S(1)}, ...), condition=%wide.region_11.12_spmd.clone, body=%wide.region_8.11_spmd.clone.sunk | while | flops 17236612 | bytes 707770 | solution.py:41
  160.2 17.5 %all-gather.11 = f32[16,1,128]{2,1,0:T(1,128)S(1)} all-gather(f32[1,1,128]{2,1,0:T(1,128)S(1)} %add_bitcast_fusion.1), channel_id=1, replica_groups=mesh['pa'=16,'pb'=2] {'pa'}, dimensions={0}, use_global_device_ids=true | all-gather | bytes 8704 | tf_op jit(solution)/shard_map/all_gather | solution.py:123
  177.7 2.4 while.114
  180.1 4.2 %all-gather.12 = f32[2,1,256]{2,1,0:T(1,128)S(1)} all-gather(f32[1,1,256]{2,1,0:T(1,128)S(1)} %bitcast.97), channel_id=4, replica_groups=mesh['pa'=16,'pb'=2] {'pb'}, dimensions={0}, use_global_device_ids=true | all-gather | bytes 3072 | tf_op jit(solution)/shard_map/all_gather | solution.py:14
  184.4 4.2 %all-gather.13 = f32[2,1,256]{2,1,0:T(1,128)S(1)} all-gather(f32[1,1,256]{2,1,0:T(1,128)S(1)} %bitcast.105), channel_id=5, replica_groups=mesh['pa'=16,'pb'=2] {'pb'}, dimensions={0}, use_global_device_ids=true | all-gather | bytes 3072 | tf_op jit(solution)/shard_map/all_gather | solution.py:14
  188.6 18.8 %all-gather.14 = f32[16,1,256]{2,1,0:T(1,128)S(1)} all-gather(f32[1,1,256]{2,1,0:T(1,128)S(1)} %bitcast.112), channel_id=1, replica_groups=mesh['pa'=16,'pb'=2] {'pa'}, dimensions={0}, use_global_device_ids=true | all-gather | bytes 17408 | tf_op jit(solution)/shard_map/all_gather | solution.py:133
  207.4 11.5 %while.115 = (s32[]{:T(128)}, f32[128]{0:T(128)S(1)}, f32[128]{0:T(128)S(1)}, f32[4096]{0:T(1024)S(1)}, f32[128]{0:T(128)S(1)}, /*index=5*/f32[4096]{0:T(1024)S(...) while((s32[]{:T(128)}, f32[128]{0:T(128)S(1)}, ...), condition=%wide.region_19.20_spmd.clone, body=%wide.region_16.19_spmd.clone.sunk | while | flops 17236612 | bytes 707770 | solution.py:41
  219.4 17.4 %all-gather.15 = f32[16,1,128]{2,1,0:T(1,128)S(1)} all-gather(f32[1,1,128]{2,1,0:T(1,128)S(1)} %get-tuple-element.1165), channel_id=1, replica_groups=mesh['pa'=16,'pb'=2] {'pa'}, dimensions={0}, use_global_device_ids=true | all-gather | bytes 8704 | tf_op jit(solution)/shard_map/all_gather | solution.py:142
  236.9 2.4 while.116
  239.3 4.2 %all-gather.16 = f32[2,1,256]{2,1,0:T(1,128)S(1)} all-gather(f32[1,1,256]{2,1,0:T(1,128)S(1)} %bitcast.96), channel_id=6, replica_groups=mesh['pa'=16,'pb'=2] {'pb'}, dimensions={0}, use_global_device_ids=true | all-gather | bytes 3072 | tf_op jit(solution)/shard_map/all_gather | solution.py:14
  243.6 4.2 %all-gather.17 = f32[2,1,256]{2,1,0:T(1,128)S(1)} all-gather(f32[1,1,256]{2,1,0:T(1,128)S(1)} %bitcast.104), channel_id=7, replica_groups=mesh['pa'=16,'pb'=2] {'pb'}, dimensions={0}, use_global_device_ids=true | all-gather | bytes 3072 | tf_op jit(solution)/shard_map/all_gather | solution.py:14
  251.5 8.4 %reduce-scatter.2.cloned.1.call-done = bf16[128,128]{1,0:T(8,128)(2,1)} async-done(((bf16[256,128]{1,0:T(8,128)(2,1)}), bf16[128,128]{1,0:T(8,128)(2,1)}) %reduce-scatter.2.cloned.1.call-update) | async-done | bytes 32784 | tf_op jit(solution)/shard_map/reduce_scatter | solution.py:145
  (301 shorter events, 43.8 us)
Async XLA Ops:
  7.2 108.8 %copy-start.1 = (bf16[128,128]{1,0:T(8,128)(2,1)S(1)}, bf16[128,128]{1,0:T(8,128)(2,1)}, u32[]{:S(2)}) copy-start(bf16[128,128]{1,0:T(8,128)(2,1)} %param.17) | copy-start | bytes 98308
  7.2 139.6 %all-gather.20.cloned.1.call-start = ((), (), s32[]{:S(2)}) async-start(), calls=%async_computation.1 | async-start | bytes 1114112 | tf_op jit(solution)/shard_map/all_gather | solution.py:114
  7.2 7.3 %collective-permute-start = (bf16[128,128]{1,0:T(8,128)(2,1)}, bf16[128,128]{1,0:T(8,128)(2,1)S(1)}, u32[]{:S(2)}, u32[]{:S(2)}) collective-permute-start(bf16[128,128]{1,0:T(8,128)(2,1)} %param.17), channel_id=1, source_target_pairs={{0,2},{2,4},{4,6},{6,8},{8,10},{10,12},{12,14},{14,16},{16,18},{18... | collective-permute-start | bytes 98312 | tf_op jit(solution)/shard_map/ppermute | solution.py:102
  14.6 6.0 %collective-permute-start.1 = (bf16[128,128]{1,0:T(8,128)(2,1)S(1)}, bf16[128,128]{1,0:T(8,128)(2,1)S(1)}, u32[]{:S(2)}, u32[]{:S(2)}) collective-permute-start(bf16[128,128]{1,0:T(8,128)(2,1)S(1)} %collective-permute-done), channel_id=1, source_target_pairs={{0,2},{2,4},{4,6},{6,8},{8,10},{10,12},{12,14},{14,16},{16,18},{18... | collective-permute-start | bytes 98312 | tf_op jit(solution)/shard_map/ppermute | solution.py:102
  20.6 6.0 %collective-permute-start.2 = (bf16[128,128]{1,0:T(8,128)(2,1)S(1)}, bf16[128,128]{1,0:T(8,128)(2,1)S(1)}, u32[]{:S(2)}, u32[]{:S(2)}) collective-permute-start(bf16[128,128]{1,0:T(8,128)(2,1)S(1)} %collective-permute-done.1), channel_id=1, source_target_pairs={{0,2},{2,4},{4,6},{6,8},{8,10},{10,12},{12,14},{14,16},{16,18},{18... | collective-permute-start | bytes 98312 | tf_op jit(solution)/shard_map/ppermute | solution.py:102
  26.6 6.0 %collective-permute-start.3 = (bf16[128,128]{1,0:T(8,128)(2,1)S(1)}, bf16[128,128]{1,0:T(8,128)(2,1)S(1)}, u32[]{:S(2)}, u32[]{:S(2)}) collective-permute-start(bf16[128,128]{1,0:T(8,128)(2,1)S(1)} %collective-permute-done.2), channel_id=1, source_target_pairs={{0,2},{2,4},{4,6},{6,8},{8,10},{10,12},{12,14},{14,16},{16,18},{18... | collective-permute-start | bytes 98312 | tf_op jit(solution)/shard_map/ppermute | solution.py:102
  32.7 6.0 %collective-permute-start.4 = (bf16[128,128]{1,0:T(8,128)(2,1)S(1)}, bf16[128,128]{1,0:T(8,128)(2,1)S(1)}, u32[]{:S(2)}, u32[]{:S(2)}) collective-permute-start(bf16[128,128]{1,0:T(8,128)(2,1)S(1)} %collective-permute-done.3), channel_id=1, source_target_pairs={{0,2},{2,4},{4,6},{6,8},{8,10},{10,12},{12,14},{14,16},{16,18},{18... | collective-permute-start | bytes 98312 | tf_op jit(solution)/shard_map/ppermute | solution.py:102
  38.7 6.0 %collective-permute-start.5 = (bf16[128,128]{1,0:T(8,128)(2,1)S(1)}, bf16[128,128]{1,0:T(8,128)(2,1)S(1)}, u32[]{:S(2)}, u32[]{:S(2)}) collective-permute-start(bf16[128,128]{1,0:T(8,128)(2,1)S(1)} %collective-permute-done.4), channel_id=1, source_target_pairs={{0,2},{2,4},{4,6},{6,8},{8,10},{10,12},{12,14},{14,16},{16,18},{18... | collective-permute-start | bytes 98312 | tf_op jit(solution)/shard_map/ppermute | solution.py:102
  44.7 6.0 %collective-permute-start.6 = (bf16[128,128]{1,0:T(8,128)(2,1)S(1)}, bf16[128,128]{1,0:T(8,128)(2,1)S(1)}, u32[]{:S(2)}, u32[]{:S(2)}) collective-permute-start(bf16[128,128]{1,0:T(8,128)(2,1)S(1)} %collective-permute-done.5), channel_id=1, source_target_pairs={{0,2},{2,4},{4,6},{6,8},{8,10},{10,12},{12,14},{14,16},{16,18},{18... | collective-permute-start | bytes 98312 | tf_op jit(solution)/shard_map/ppermute | solution.py:102
  50.8 6.0 %collective-permute-start.7 = (bf16[128,128]{1,0:T(8,128)(2,1)S(1)}, bf16[128,128]{1,0:T(8,128)(2,1)S(1)}, u32[]{:S(2)}, u32[]{:S(2)}) collective-permute-start(bf16[128,128]{1,0:T(8,128)(2,1)S(1)} %collective-permute-done.6), channel_id=1, source_target_pairs={{0,2},{2,4},{4,6},{6,8},{8,10},{10,12},{12,14},{14,16},{16,18},{18... | collective-permute-start | bytes 98312 | tf_op jit(solution)/shard_map/ppermute | solution.py:102
  56.8 6.0 %collective-permute-start.8 = (bf16[128,128]{1,0:T(8,128)(2,1)S(1)}, bf16[128,128]{1,0:T(8,128)(2,1)S(1)}, u32[]{:S(2)}, u32[]{:S(2)}) collective-permute-start(bf16[128,128]{1,0:T(8,128)(2,1)S(1)} %collective-permute-done.7), channel_id=1, source_target_pairs={{0,2},{2,4},{4,6},{6,8},{8,10},{10,12},{12,14},{14,16},{16,18},{18... | collective-permute-start | bytes 98312 | tf_op jit(solution)/shard_map/ppermute | solution.py:102
  62.9 6.0 %collective-permute-start.9 = (bf16[128,128]{1,0:T(8,128)(2,1)S(1)}, bf16[128,128]{1,0:T(8,128)(2,1)S(1)}, u32[]{:S(2)}, u32[]{:S(2)}) collective-permute-start(bf16[128,128]{1,0:T(8,128)(2,1)S(1)} %collective-permute-done.8), channel_id=1, source_target_pairs={{0,2},{2,4},{4,6},{6,8},{8,10},{10,12},{12,14},{14,16},{16,18},{18... | collective-permute-start | bytes 98312 | tf_op jit(solution)/shard_map/ppermute | solution.py:102
  68.9 6.0 %collective-permute-start.10 = (bf16[128,128]{1,0:T(8,128)(2,1)S(1)}, bf16[128,128]{1,0:T(8,128)(2,1)S(1)}, u32[]{:S(2)}, u32[]{:S(2)}) collective-permute-start(bf16[128,128]{1,0:T(8,128)(2,1)S(1)} %collective-permute-done.9), channel_id=1, source_target_pairs={{0,2},{2,4},{4,6},{6,8},{8,10},{10,12},{12,14},{14,16},{16,18},{18... | collective-permute-start | bytes 98312 | tf_op jit(solution)/shard_map/ppermute | solution.py:102
  74.9 6.0 %collective-permute-start.11 = (bf16[128,128]{1,0:T(8,128)(2,1)S(1)}, bf16[128,128]{1,0:T(8,128)(2,1)S(1)}, u32[]{:S(2)}, u32[]{:S(2)}) collective-permute-start(bf16[128,128]{1,0:T(8,128)(2,1)S(1)} %collective-permute-done.10), channel_id=1, source_target_pairs={{0,2},{2,4},{4,6},{6,8},{8,10},{10,12},{12,14},{14,16},{16,18},{18... | collective-permute-start | bytes 98312 | tf_op jit(solution)/shard_map/ppermute | solution.py:102
  81.0 6.0 %collective-permute-start.12 = (bf16[128,128]{1,0:T(8,128)(2,1)S(1)}, bf16[128,128]{1,0:T(8,128)(2,1)S(1)}, u32[]{:S(2)}, u32[]{:S(2)}) collective-permute-start(bf16[128,128]{1,0:T(8,128)(2,1)S(1)} %collective-permute-done.11), channel_id=1, source_target_pairs={{0,2},{2,4},{4,6},{6,8},{8,10},{10,12},{12,14},{14,16},{16,18},{18... | collective-permute-start | bytes 98312 | tf_op jit(solution)/shard_map/ppermute | solution.py:102
  86.5 173.3 %reduce-scatter.2.cloned.1.call-start = ((), (), s32[]{:S(2)}) async-start(), calls=%async_computation.2 | async-start | bytes 98304 | tf_op jit(solution)/shard_map/reduce_scatter | solution.py:145
  87.0 6.0 %collective-permute-start.13 = (bf16[128,128]{1,0:T(8,128)(2,1)S(1)}, bf16[128,128]{1,0:T(8,128)(2,1)S(1)}, u32[]{:S(2)}, u32[]{:S(2)}) collective-permute-start(bf16[128,128]{1,0:T(8,128)(2,1)S(1)} %collective-permute-done.12), channel_id=1, source_target_pairs={{0,2},{2,4},{4,6},{6,8},{8,10},{10,12},{12,14},{14,16},{16,18},{18... | collective-permute-start | bytes 98312 | tf_op jit(solution)/shard_map/ppermute | solution.py:102
  93.0 22.7 %collective-permute-start.14 = (bf16[128,128]{1,0:T(8,128)(2,1)S(1)}, bf16[128,128]{1,0:T(8,128)(2,1)S(1)}, u32[]{:S(2)}, u32[]{:S(2)}) collective-permute-start(bf16[128,128]{1,0:T(8,128)(2,1)S(1)} %collective-permute-done.13), channel_id=1, source_target_pairs={{0,2},{2,4},{4,6},{6,8},{8,10},{10,12},{12,14},{14,16},{16,18},{18... | collective-permute-start | bytes 98312 | tf_op jit(solution)/shard_map/ppermute | solution.py:102
  116.0 0.8 copy-start
  148.6 11.6 %copy-start.3 = (f32[128]{0:T(128)S(1)}, f32[128]{0:T(128)}, u32[]{:S(2)}) copy-start(f32[128]{0:T(128)} %param.19) | copy-start | bytes 1540
  247.8 12.1 %copy-start.2 = (f32[128,128]{1,0:T(8,128)S(1)}, f32[128,128]{1,0:T(8,128)}, u32[]{:S(2)}) copy-start(f32[128,128]{1,0:T(8,128)} %param.16) | copy-start | bytes 196612
Sparse Core Ops, SparseCore 0:
  86.6 38.2 all-gather.19
  251.0 8.8 reduce-scatter.1
